TPU v7x, 512 devices: a 8x2x16 block of a 8x8x16 slice. The times are simulated.
512 devices in a mesh: grp: 2 (over y), ep: 128 (over x, z), tp: 2 (over core).
Axes of the slice: x: 8, y: 2, z: 16, core: 2. Of those that a mesh axis runs over, the one named last changes fastest.
The devices are a block of a 8x8x16 slice.
Arguments:
- queries: bfloat16 [16384, 16, 576], P(('grp', 'ep'), 'tp'), parts along dimension 0, may hold values from -450 to 450
- latent_cache: bfloat16 [768, 512, 576], P(('grp', 'ep'), 'tp'), parts along dimension 0, may hold values from -6 to 6
- residual: bfloat16 [16384, 2048], P(('grp', 'ep')), parts along dimension 0, may hold values from -8 to 8
- token_request: int32 [16384], P(('grp', 'ep')), parts along dimension 0, may hold values from 0 to 2, as said below
- token_visible: int32 [16384], P(('grp', 'ep')), parts along dimension 0, may hold values from 1 to 512, as said below
- value_proj: bfloat16 [16, 512, 128], P('tp', 'ep'), may hold values from -0.25 to 0.25
- out_proj: bfloat16 [2048, 2048], P('tp', 'ep'), may hold values from -0.125 to 0.125
- norm_gain: float32 [2048], replicated, may hold values from 0.1 to 1.9
- router: bfloat16 [2048, 64], replicated, may hold values from -0.0390625 to 0.0390625
- expert_ids: int32 [16384, 6], P(('grp', 'ep')), parts along dimension 0, may hold values from 0 to 63, all different within a row; in each aligned block of 64 rows (0 to 63, 64 to 127, ...) at most 8 rows name the same one
- gate_weight: bfloat16 [128, 2048, 384], P('ep', None, 'tp'), may hold values from -0.125 to 0.125
- up_weight: bfloat16 [128, 2048, 384], P('ep', None, 'tp'), may hold values from -0.125 to 0.125
- down_weight: bfloat16 [128, 384, 2048], P('ep', 'tp'), may hold values from -0.21875 to 0.21875
Outputs:
- hidden: bfloat16 [16384, 2048], P(('grp', 'ep'), 'tp'), parts along dimension 0
- expert_out: bfloat16 [16384, 2048], P(('grp', 'ep'), 'tp'), parts along dimension 0
There are 2 independent parts, one for each index of `grp`. A program takes and returns all parts, laid end to end along the dimension named above; an argument that names none is the same for every part. Nothing has to cross between parts.
Inputs may be any that keep to these rules, and one draw needn't show every extreme that they name: `token_request`: in each ep block, 62 tokens belong to request 0, a prefill span, and each other request has exactly one token; the tokens' order in the block is arbitrary. `token_visible`: the span's tokens read consecutive counts s + 1 to s + 62; 512 is reached in every draw. `expert_ids`: each row names 6 different experts; among the 64 tokens of one ep index no expert is named by more than 8 tokens, and this bound is reached.
All inputs are finite; a program needn't handle non-finite values.
Results may differ from a plain program's by a relative error of at most 0.018.
Values may be sent and summed in bfloat16 or wider, within the bound.
A program may use at most 64 MiB of HBM per device.

v0:
```python
import jax
import jax.numpy as jnp
from jax import lax
from jax.sharding import Mesh
from jax.sharding import PartitionSpec as P

LATENT = 512
VDIM = 128
EXPERTS = 64
TOPK = 6
GROUPS = 2
CAP = 8
PIECES = 128
EP = ("ep_0", "ep_1")
GRP_EP = ("grp", "ep_0", "ep_1")
score_scale = 192.0 ** (-0.5)
epsilon = 1e-06


def from_everyone(value, axis):
    peers = lax.axis_size(axis)
    return lax.all_to_all(
        jnp.broadcast_to(value[None], (peers, *value.shape)), axis, 0, 0, tiled=True
    )


def laid_out(pieces, dim):
    lengths = list(pieces.shape[1:])
    lengths[dim] *= pieces.shape[0]
    return jnp.moveaxis(pieces, 0, dim).reshape(lengths)


def collect(value, axis, dim):
    pieces = from_everyone(value, axis)
    return laid_out(pieces, dim)


def of_everyone(value, axis):
    return from_everyone(value, axis).max(axis=0)


def split_up(value, dim, peers):
    before, after = (value.shape[:dim], value.shape[dim + 1 :])
    return jnp.moveaxis(value.reshape(*before, peers, -1, *after), dim, 0)


def sent_and_summed(value, axis, dim):
    peers = lax.axis_size(axis)
    pieces = lax.all_to_all(split_up(value, dim, peers), axis, 0, 0, tiled=True)
    return jnp.sum(pieces, axis=0)


def sent_together(arrays, axis, dim, along):
    columns = [a.reshape(*a.shape[:along], -1) for a in arrays]
    both = jnp.concatenate(columns, axis=along)
    result, at, outs = (sent_and_summed(both, axis, dim), 0, [])
    for a, column in zip(arrays, columns):
        piece = result[..., at : at + column.shape[along]]
        outs.append(piece.reshape(*piece.shape[:along], *a.shape[along:]))
        at += column.shape[along]
    return tuple(outs)


def stacked_from(value, axes, order):
    pieces = value[None]
    for k in order:
        pieces = lax.all_gather(pieces, axes[k], axis=0, tiled=True)
    carried = [lax.axis_size(axes[k]) for k in reversed(order)]
    pieces = pieces.reshape(*carried, *value.shape)
    turned = sorted(range(len(order)), key=lambda place: order[len(order) - 1 - place])
    return pieces.transpose(*turned, *range(len(order), pieces.ndim)).reshape(-1, *value.shape)


def whole_of(value, axes, order, dim):
    return laid_out(stacked_from(value, axes, order), dim)


def over_copies(value, axis):
    everything = from_everyone(value, axis)
    return jnp.sum(everything, axis=0)


def masked_scores(queries, block_rows, token_request, token_visible, offset):
    per_request = block_rows.shape[1]
    flat_rows = block_rows.reshape(-1, block_rows.shape[2])
    scores = (
        jnp.einsum("thc,kc->thk", queries, flat_rows, preferred_element_type=jnp.float32)
        * score_scale
    )
    column = jnp.arange(flat_rows.shape[0], dtype=jnp.int32)
    owner_id = column // per_request
    position = column % per_request + offset
    allowed = (owner_id[None, :] == token_request[:, None]) & (
        position[None, :] < token_visible[:, None]
    )
    return (jnp.where(allowed[:, None, :], scores, -jnp.inf), flat_rows)


def weighted_rows(scores, row_peak, flat_rows):
    weights = jnp.exp(scores - row_peak[:, :, None]).astype(jnp.bfloat16)
    totals = jnp.sum(weights.astype(jnp.float32), axis=2)
    summed = jnp.einsum(
        "thk,kc->thc", weights, flat_rows[:, :LATENT], preferred_element_type=jnp.float32
    )
    return (summed, totals)


def expert_block(arrived, gate_weight, up_weight, down_weight):
    gate_vals = jnp.einsum("prd,pdf->prf", arrived, gate_weight, preferred_element_type=jnp.float32)
    up_vals = jnp.einsum("prd,pdf->prf", arrived, up_weight, preferred_element_type=jnp.float32)
    activated = (jax.nn.silu(gate_vals) * up_vals).astype(jnp.bfloat16)
    return jnp.einsum(
        "prf,pfd->prd", activated, down_weight, preferred_element_type=jnp.float32
    ).astype(jnp.bfloat16)


def body(
    queries,
    latent_cache,
    residual,
    token_request,
    token_visible,
    value_proj,
    out_proj,
    norm_gain,
    router,
    expert_ids,
    gate_weight,
    up_weight,
    down_weight,
):
    all_heads = collect(queries, "tp", 1)
    offset = lax.axis_index("tp") * latent_cache.shape[1]
    scores, flat_rows = masked_scores(all_heads, latent_cache, token_request, token_visible, offset)
    row_peak = of_everyone(jnp.max(scores, axis=2), "tp")
    part_sum, part_total = weighted_rows(scores, row_peak, flat_rows)
    summed, totals = sent_together((part_sum, part_total), "tp", 1, 2)
    context = (summed / totals[:, :, None]).astype(jnp.bfloat16)
    tokens_here = context.shape[0]
    heads_here = context.shape[1]
    head_values = jnp.einsum(
        "thl,hlv->thv",
        context,
        whole_of(value_proj, EP, (0, 1), 1),
        preferred_element_type=jnp.float32,
    )
    heads_out = head_values.astype(jnp.bfloat16).reshape(tokens_here, heads_here * VDIM)
    attention_part = jnp.dot(
        heads_out, whole_of(out_proj, EP, (0, 1), 1), preferred_element_type=jnp.float32
    )
    attention = over_copies(attention_part, "tp")
    hidden = (residual.astype(jnp.float32) + attention).astype(jnp.bfloat16)
    hidden_wide = hidden.astype(jnp.float32)
    normed = (
        hidden_wide
        * lax.rsqrt(jnp.mean(hidden_wide * hidden_wide, axis=1, keepdims=True) + epsilon)
        * norm_gain
    ).astype(jnp.bfloat16)
    logits = jnp.dot(normed, router, preferred_element_type=jnp.float32)
    gate_share = jax.nn.softmax(jnp.take_along_axis(logits, expert_ids, axis=1), axis=1).astype(
        jnp.bfloat16
    )
    flat_ids = expert_ids.reshape(-1)
    position_id = jnp.arange(flat_ids.shape[0], dtype=jnp.int32)
    earlier = (flat_ids[:, None] == flat_ids[None, :]) & (
        position_id[None, :] < position_id[:, None]
    )
    slot_ids = (flat_ids * CAP + jnp.sum(earlier.astype(jnp.int32), axis=1)).reshape(
        tokens_here, TOPK
    )
    targets = jnp.arange(EXPERTS * CAP, dtype=jnp.int32)
    matches = slot_ids[:, :, None] == targets[None, None, :]
    picker = jnp.any(matches, axis=1).T.astype(jnp.bfloat16)
    model_width = normed.shape[1]
    mixing = jnp.sum(
        jnp.where(matches, gate_share[:, :, None], jnp.zeros((), jnp.bfloat16)), axis=1
    )
    mixing = jnp.broadcast_to(
        mixing.reshape(tokens_here, EXPERTS, 1, CAP), (tokens_here, EXPERTS, GROUPS, CAP)
    ).reshape(tokens_here, PIECES * CAP)
    core_count = lax.axis_size("tp")
    half_width = model_width // core_count
    core_start = lax.axis_index("tp") * half_width
    normed_share = lax.dynamic_slice_in_dim(normed, core_start, half_width, 1)
    outgoing = jnp.dot(picker, normed_share, preferred_element_type=jnp.float32).astype(
        jnp.bfloat16
    )
    outgoing = jnp.broadcast_to(
        outgoing.reshape(EXPERTS, 1, CAP, half_width), (EXPERTS, GROUPS, CAP, half_width)
    ).reshape(PIECES, CAP, half_width)
    arrived_share = lax.all_to_all(outgoing, EP, split_axis=0, concat_axis=1, tiled=True)
    arrived = lax.all_gather(arrived_share, "tp", axis=2, tiled=True)
    partial_out = expert_block(arrived, gate_weight, up_weight, down_weight)
    swapped = lax.all_to_all(partial_out[None], "tp", split_axis=3, concat_axis=0, tiled=True)
    returned = lax.all_to_all(swapped, EP, split_axis=2, concat_axis=1, tiled=True)
    returned = returned.reshape(core_count, PIECES * CAP, half_width)
    routed = jnp.einsum("tk,qkd->td", mixing, returned, preferred_element_type=jnp.float32)
    expert_out = routed.astype(jnp.bfloat16)
    hidden_part = lax.dynamic_slice_in_dim(hidden, core_start, half_width, 1)
    return (hidden_part, expert_out)


def solution(mesh):
    finer = Mesh(
        mesh.devices.reshape(mesh.shape["grp"], 8, 16, mesh.shape["tp"]),
        ("grp", "ep_0", "ep_1", "tp"),
    )
    in_specs = (
        P(GRP_EP, "tp", None),
        P(GRP_EP, "tp", None),
        P(GRP_EP, None),
        P(GRP_EP),
        P(GRP_EP),
        P("tp", EP, None),
        P("tp", EP),
        P(),
        P(),
        P(GRP_EP, None),
        P(EP, None, "tp"),
        P(EP, None, "tp"),
        P(EP, "tp", None),
    )
    out_specs = (P(GRP_EP, "tp"), P(GRP_EP, "tp"))
    return jax.shard_map(body, mesh=finer, in_specs=in_specs, out_specs=out_specs, check_vma=False)
```

profile of v0, /device:TPU:320, one launch (start us, length us, event | category | flops | bytes accessed | tf_op | source)
XLA Modules:
  0.0 692.1 jit_solution(127817837888464356)
XLA Ops:
  7.3 26.9 %all-gather = bf16[64,4,128]{2,1,0:T(4,128)(2,1)S(1)} all-gather(bf16[8,4,128]{2,1,0:T(4,128)(2,1)} %param.18), channel_id=2, replica_groups=mesh['grp'=2,'ep_0'=8,'ep_1'=16,'tp'=2] {'ep_0'}, dimensions={0}, use_global_device_ids=true | all-gather | bytes 73728 | tf_op jit(solution)/shard_map/all_gather | solution.py:67
  34.1 0.6 copy.183
  34.9 25.1 %all-gather.1 = bf16[8192,16]{0,1:T(8,128)(2,1)S(1)} all-gather(bf16[1024,16]{0,1:T(8,128)(2,1)} %param.19), channel_id=3, replica_groups=mesh['grp'=2,'ep_0'=8,'ep_1'=16,'tp'=2] {'ep_0'}, dimensions={0}, use_global_device_ids=true | all-gather | bytes 294912 | tf_op jit(solution)/shard_map/all_gather | solution.py:67
  60.0 0.9 copy.205
  61.0 2.3 broadcast_in_dim.49
  63.2 3.7 all-to-all-start
  66.9 1.5 copy.173
  68.5 0.1 compare_and_fusion
  68.6 0.6 all-to-all-done
  69.1 3.2 fusion.4
  72.5 3.7 all_to_all.59
  76.2 0.5 broadcast.146
  76.7 0.7 reduce.3
  77.5 2.9 convert_reduce_fusion.1
  80.5 0.3 copy.179
  80.8 3.1 convolution_bitcast_fusion
  83.9 1.8 maximum_bitcast_fusion
  85.6 4.0 all-to-all-start.2
  89.7 0.3 all-gather.10.cloned.1.call-start
  90.1 0.1 eq.50
  90.2 0.2 convert_reduce_fusion.2
  90.5 0.2 reduce_sum.81
  90.7 2.2 all-to-all-done.2
  92.9 1.4 reduce_sum.78
  94.2 1.0 slice.16
  95.2 0.4 copy.198
  95.7 0.2 fusion.27
  95.8 1.4 fusion.16
  97.2 36.4 %all-gather.6.cloned.1.call-done = bf16[128,8,4,128]{3,1,2,0:T(8,128)(2,1)} async-done(((bf16[8,8,4,128]{3,1,2,0:T(8,128)(2,1)}), bf16[128,8,4,128]{3,1,2,0:T(8,128)(2,1)}) %all-gather.6.cloned.1.call-update) | async-done | bytes 1048592 | tf_op jit(solution)/shard_map/all_gather | solution.py:67
  133.6 1.8 copy.184
  135.4 0.4 fusion.15
  135.8 76.6 %all-gather.8.cloned.1.call-done = bf16[128,1024,16]{1,0,2:T(8,128)(2,1)} async-done(((bf16[8,1024,16]{1,0,2:T(8,128)(2,1)}), bf16[128,1024,16]{1,0,2:T(8,128)(2,1)}) %all-gather.8.cloned.1.call-update) | async-done | bytes 4194320 | tf_op jit(solution)/shard_map/all_gather | solution.py:67
  212.5 4.5 copy.188
  217.0 1.4 fusion.36
  218.4 0.1 broadcast_in_dim.89
  218.5 4.6 all_to_all.60
  223.1 0.1 reduce_sum.79
  223.2 0.2 fusion.30
  223.4 0.1 fusion.32
  223.5 0.5 fusion.5
  224.0 0.3 broadcast_in_dim.96
  224.3 118.1 %all_to_all.61 = bf16[128,8,1024]{2,1,0:T(8,128)(2,1)} all-to-all(bf16[128,8,1024]{2,1,0:T(8,128)(2,1)S(1)} %bitcast.107), channel_id=1, replica_groups=mesh['grp'=2,'ep_0'=8,'ep_1'=16,'tp'=2] {'ep_0','ep_1'}, dimensions={0} | all-to-all | bytes 4194304 | tf_op jit(solution)/shard_map/all_to_all | solution.py:191
  342.5 14.4 %all-gather.10.cloned.1.call-done = bf16[1,1024,2048]{2,1,0:T(8,128)(2,1)} async-done(((bf16[1,1024,1024]{2,1,0:T(8,128)(2,1)}), bf16[1,1024,2048]{2,1,0:T(8,128)(2,1)}) %all-gather.10.cloned.1.call-update) | async-done | bytes 4194320 | tf_op jit(solution)/shard_map/all_gather | solution.py:192
  356.9 4.6 fusion.2
  361.5 7.3 %convert_bitcast_fusion = bf16[1,1,1024,2048]{3,2,1,0:T(8,128)(2,1)} fusion(bf16[1,192,2048]{2,1,0:T(8,128)(2,1)S(1)} %copy-done, bf16[1,1024,2048]{2,1,0:T(8,128)(2,1)} %all-gather.10.cloned.1.call-done, bf16[1,2048,192]{1,2,0:T(8,128)(2,1)} %param.24, f32[1024,192]{0,1:T(8,128)} %fusion.2), kind=kOutput, calls=%fused_computation.6 | convolution fusion | flops 1613889536 | bytes 10747904 | tf_op jit(solution)/shard_map/prf,pfd->prd/dot_general | solution.py:112
  368.8 20.6 %copy.194 = bf16[1,1,1024,2048]{2,1,0,3:T(2,128)(2,1)} copy(bf16[1,1,1024,2048]{3,2,1,0:T(8,128)(2,1)} %convert_bitcast_fusion) | data formatting | bytes 8388608 | tf_op jit(solution)/shard_map/broadcast_in_dim | solution.py:194
  389.4 0.5 broadcast.147
  389.9 26.0 %reduce.4 = bf16[2048,1024]{1,0:T(8,128)(2,1)} reduce(bf16[2048,1,1,1024]{3,2,1,0:T(2,128)(2,1)} %bitcast.102, bf16[]{:T(256)} %broadcast.147), dimensions={1,2}, to_apply=%bitcast.85.reduce_sub_computation | reduce | bytes 8388610
  415.9 5.9 reshape.241
  421.8 11.9 %all_to_all.62 = bf16[2,2,524288]{2,1,0:T(2,128)(2,1)} all-to-all(bf16[2,2,524288]{2,1,0:T(2,128)(2,1)} %reshape.241), channel_id=1, replica_groups=mesh['grp'=2,'ep_0'=8,'ep_1'=16,'tp'=2] {'tp'}, dimensions={0} | all-to-all | bytes 8388608 | tf_op jit(solution)/shard_map/all_to_all | solution.py:194
  433.7 7.1 %reshape.242 = bf16[2048,1,1,1024]{3,2,1,0:T(2,128)(2,1)} reshape(bf16[2,2,524288]{2,1,0:T(2,128)(2,1)} %all_to_all.62) | data formatting | bytes 8388608
  440.8 7.1 %copy.200 = bf16[1,1,1024,2048]{2,3,0,1:T(8,128)(2,1)} copy(bf16[1,1,1024,2048]{2,1,0,3:T(2,128)(2,1)} %bitcast.103) | data formatting | bytes 8388608
  447.8 11.3 %copy.195 = bf16[2,1,1024,1024]{3,0,1,2:T(2,128)(2,1)} copy(bf16[2,1,1024,1024]{2,3,0,1:T(8,128)(2,1)} %bitcast.104) | data formatting | bytes 8388608 | tf_op jit(solution)/shard_map/all_to_all | solution.py:194
  459.1 21.4 %all-to-all-start.6 = ((bf16[2,1,1024,1024]{3,0,1,2:T(2,128)(2,1)}), bf16[2,1,1024,1024]{3,0,1,2:T(2,128)(2,1)}, u32[]{:S(2)}, u32[]{:S(2)}) async-start(bf16[2,1,1024,1024]{3,0,1,2:T(2,128)(2,1)} %copy.195), calls=%async_computation.6 | async-start | bytes 8388608 | tf_op jit(solution)/shard_map/all_to_all | solution.py:195
  480.7 0.1 reshape.224
  480.8 0.2 fusion.54
  481.0 2.9 gather_fusion
  483.9 0.1 reshape.227
  484.2 0.2 fusion.34
  484.4 0.1 copy.193
  484.5 0.7 constant_dynamic-slice_fusion
  485.2 186.6 %all-to-all-done.6 = bf16[2,1,1024,1024]{3,0,1,2:T(2,128)(2,1)} async-done(((bf16[2,1,1024,1024]{3,0,1,2:T(2,128)(2,1)}), bf16[2,1,1024,1024]{3,0,1,2:T(2,128)(2,1)}, u32[]{:S(2)}, u32[]{:S(2)}) %all-to-all-start.6) | async-done | bytes 4194336 | tf_op jit(solution)/shard_map/all_to_all | solution.py:195
  671.8 12.4 %convert_reduce_fusion = bf16[1024,1024]{1,0:T(8,128)(2,1)S(1)} fusion(bf16[2,1,1024,1024]{3,0,1,2:T(2,128)(2,1)} %all-to-all-done.6), kind=kLoop, calls=%fused_computation.1 | loop fusion | flops 3145728 | bytes 6291456 | tf_op jit(solution)/shard_map/tk,qkd->td/reduce_sum | solution.py:197
  684.2 1.2 fusion.55
  (42 shorter events, 1.2 us)
Async XLA Ops:
  7.2 354.3 %copy-start = (bf16[1,192,2048]{2,1,0:T(8,128)(2,1)S(1)}, bf16[1,192,2048]{2,1,0:T(8,128)(2,1)}, u32[]{:S(2)}) copy-start(bf16[1,192,2048]{2,1,0:T(8,128)(2,1)} %param.25) | copy-start | bytes 2359300
  7.2 126.4 %all-gather.6.cloned.1.call-start = ((), (), s32[]{:S(2)}) async-start(), calls=%async_computation.7 | async-start | bytes 1114112 | tf_op jit(solution)/shard_map/all_gather | solution.py:67
  34.8 177.6 %all-gather.8.cloned.1.call-start = ((), (), s32[]{:S(2)}) async-start(), calls=%async_computation.8 | async-start | bytes 4456448 | tf_op jit(solution)/shard_map/all_gather | solution.py:67
  60.9 7.5 %copy-start.6 = (s32[64]{0:T(128)S(1)}, s32[64]{0:T(128)}, u32[]{:S(2)}) copy-start(s32[64]{0:T(128)} %param.17) | copy-start | bytes 772
  60.9 7.5 %copy-start.7 = (s32[64]{0:T(128)S(1)}, s32[64]{0:T(128)}, u32[]{:S(2)}) copy-start(s32[64]{0:T(128)} %param.16) | copy-start | bytes 772
  63.2 5.9 all-to-all-start
  85.6 4.4 copy-start.4
  85.6 7.2 %all-to-all-start.2 = ((f32[2,64,8,513]{3,2,1,0:T(8,128)}), f32[2,64,8,513]{3,2,1,0:T(8,128)S(1)}, u32[]{:S(2)}, u32[]{:S(2)}) async-start(f32[2,64,8,513]{3,2,1,0:T(8,128)} %maximum_bitcast_fusion), calls=%async_computation.2 | async-start | bytes 5242880 | tf_op jit(solution)/shard_map/all_to_all | solution.py:49
  89.7 267.2 %all-gather.10.cloned.1.call-start = ((), (), s32[]{:S(2)}) async-start(), calls=%async_computation.9 | async-start | bytes 6291456 | tf_op jit(solution)/shard_map/all_gather | solution.py:192
  218.4 4.8 copy-start.3
  218.4 5.0 copy-start.5
  224.3 132.6 %copy-start.8 = (bf16[1,2048,192]{1,2,0:T(8,128)(2,1)S(1)}, bf16[1,2048,192]{1,2,0:T(8,128)(2,1)}, u32[]{:S(2)}) copy-start(bf16[1,2048,192]{1,2,0:T(8,128)(2,1)} %param.23) | copy-start | bytes 2359300
  459.1 21.7 %copy-start.2 = (bf16[2048,64]{0,1:T(8,128)(2,1)S(1)}, bf16[2048,64]{0,1:T(8,128)(2,1)}, u32[]{:S(2)}) copy-start(bf16[2048,64]{0,1:T(8,128)(2,1)} %param.21) | copy-start | bytes 786436
  459.1 212.7 %all-to-all-start.6 = ((bf16[2,1,1024,1024]{3,0,1,2:T(2,128)(2,1)}), bf16[2,1,1024,1024]{3,0,1,2:T(2,128)(2,1)}, u32[]{:S(2)}, u32[]{:S(2)}) async-start(bf16[2,1,1024,1024]{3,0,1,2:T(2,128)(2,1)} %copy.195), calls=%async_computation.6 | async-start | bytes 8388608 | tf_op jit(solution)/shard_map/all_to_all | solution.py:195
  484.5 200.9 %copy-start.1 = (bf16[1,192,2048]{2,1,0:T(8,128)(2,1)S(1)}, bf16[1,192,2048]{2,1,0:T(8,128)(2,1)}, u32[]{:S(2)}) copy-start(bf16[1,192,2048]{2,1,0:T(8,128)(2,1)} %param.25) | copy-start | bytes 2359300
Sparse Core Ops, SparseCore 0:
  34.9 98.6 all-gather.5
  135.7 76.7 all-gather.7
  342.6 14.2 all-gather.9
where the time goes:
time: 700 us; the launch traced here: 692 us
  waiting for transfers between devices  317 us (45%)
  blocking collectives  190 us (27%)
  local copies, waits for them, and re-layouts  71.6 us (10%)
  other arithmetic  47.6 us (7%)
  starting transfers between devices  29.5 us (4%)
  matrix products  21.9 us (3%)
  between operations  14.3 us (2%)
    all_to_all x1, waiting for transfers between devices, body(): lax.all_to_all(swapped, EP, split_axis=2, concat_axis=1, tiled=True)  187 us
    all_to_all x1, blocking collectives, body(): lax.all_to_all(outgoing, EP, split_axis=0, concat_axis=1, tiled=True)  118 us
    all_gather x2, waiting for transfers between devices, stacked_from(): pieces = lax.all_gather(pieces, axes[k], axis=0, tiled=True)  113 us
    all_gather x2, blocking collectives, stacked_from(): pieces = lax.all_gather(pieces, axes[k], axis=0, tiled=True)  52 us
    unnamed x1, other arithmetic  26 us
    unnamed x28, local copies, waits for them, and re-layouts  23.3 us
    all_to_all x1, starting transfers between devices, body(): lax.all_to_all(swapped, EP, split_axis=2, concat_axis=1, tiled=True)  21.4 us
    broadcast_in_dim x1, local copies, waits for them, and re-layouts, body(): partial_out[None]  20.6 us
  transfers between devices with their start and end apart: 6, of which 6 were waited for; matrix products, arithmetic and copies ran while one was open for 4% of the time, Pallas kernels for 0%

commit v1 on v0

--- a/solution.py
+++ b/solution.py
@@ -188,7 +188,9 @@
     outgoing = jnp.broadcast_to(
         outgoing.reshape(EXPERTS, 1, CAP, half_width), (EXPERTS, GROUPS, CAP, half_width)
     ).reshape(PIECES, CAP, half_width)
-    arrived_share = lax.all_to_all(outgoing, EP, split_axis=0, concat_axis=1, tiled=True)
+    arrived_share = jnp.concatenate(
+        lax.all_to_all(jnp.stack(jnp.split(outgoing, lax.axis_size(EP), axis=0)), EP, 0, 0), axis=1
+    )
     arrived = lax.all_gather(arrived_share, "tp", axis=2, tiled=True)
     partial_out = expert_block(arrived, gate_weight, up_weight, down_weight)
     swapped = lax.all_to_all(partial_out[None], "tp", split_axis=3, concat_axis=0, tiled=True)

time: 700 us -> 701 us (level)
    unnamed x28 -> x155, local copies, waits for them, and re-layouts: 23.3 us -> 23.7 us
where the time goes in v1:
time: 701 us; the launch traced here: 693 us
  waiting for transfers between devices  317 us (45%)
  blocking collectives  190 us (27%)
  local copies, waits for them, and re-layouts  72 us (10%)
  other arithmetic  47.6 us (7%)
  starting transfers between devices  29.9 us (4%)
  matrix products  21.9 us (3%)
  between operations  15.3 us (2%)
    all_to_all x1, waiting for transfers between devices, body(): lax.all_to_all(swapped, EP, split_axis=2, concat_axis=1, tiled=True)  187 us
    all_to_all x1, blocking collectives, body(): lax.all_to_all(jnp.stack(jnp.split(outgoing, lax.axis_size(EP), axis=0)),...  118 us
    all_gather x2, waiting for transfers between devices, stacked_from(): pieces = lax.all_gather(pieces, axes[k], axis=0, tiled=True)  113 us
    all_gather x2, blocking collectives, stacked_from(): pieces = lax.all_gather(pieces, axes[k], axis=0, tiled=True)  52 us
    unnamed x1, other arithmetic  26 us
    unnamed x155, local copies, waits for them, and re-layouts  23.7 us
    all_to_all x1, starting transfers between devices, body(): lax.all_to_all(swapped, EP, split_axis=2, concat_axis=1, tiled=True)  21.4 us
    broadcast_in_dim x1, local copies, waits for them, and re-layouts, body(): partial_out[None]  20.6 us
  transfers between devices with their start and end apart: 6, of which 6 were waited for; matrix products, arithmetic and copies ran while one was open for 4% of the time, Pallas kernels for 0%

profile of v1, /device:TPU:320, one launch (start us, length us, event | category | flops | bytes accessed | tf_op | source)
XLA Modules:
  0.0 693.4 jit_solution(1726210611363446255)
XLA Ops:
  7.3 26.9 %all-gather = bf16[64,4,128]{2,1,0:T(4,128)(2,1)S(1)} all-gather(bf16[8,4,128]{2,1,0:T(4,128)(2,1)} %param.18), channel_id=2, replica_groups=mesh['grp'=2,'ep_0'=8,'ep_1'=16,'tp'=2] {'ep_0'}, dimensions={0}, use_global_device_ids=true | all-gather | bytes 73728 | tf_op jit(solution)/shard_map/all_gather | solution.py:67
  34.1 0.6 copy.183
  34.9 25.1 %all-gather.1 = bf16[8192,16]{0,1:T(8,128)(2,1)S(1)} all-gather(bf16[1024,16]{0,1:T(8,128)(2,1)} %param.19), channel_id=3, replica_groups=mesh['grp'=2,'ep_0'=8,'ep_1'=16,'tp'=2] {'ep_0'}, dimensions={0}, use_global_device_ids=true | all-gather | bytes 294912 | tf_op jit(solution)/shard_map/all_gather | solution.py:67
  60.0 0.9 copy.205
  60.9 2.2 broadcast_in_dim.49
  63.2 3.8 all-to-all-start
  67.0 1.5 copy.173
  68.6 0.1 compare_and_fusion
  68.7 0.6 all-to-all-done
  69.3 3.2 fusion.4
  72.6 3.7 all_to_all.52
  76.3 0.5 broadcast.146
  76.8 0.7 reduce.3
  77.6 2.9 convert_reduce_fusion.1
  80.6 0.3 copy.179
  80.9 3.1 convolution_bitcast_fusion
  84.0 1.8 maximum_bitcast_fusion
  85.8 4.0 all-to-all-start.2
  89.8 0.5 all-gather.10.cloned.1.call-start
  90.4 0.1 eq.50
  90.6 0.2 convert_reduce_fusion.2
  90.8 0.1 reduce_sum.81
  91.0 2.0 all-to-all-done.2
  93.0 1.4 reduce_sum.78
  94.4 1.0 slice.16
  95.3 0.4 copy.198
  95.8 0.2 fusion.27
  96.0 1.4 fusion.16
  97.3 36.3 %all-gather.6.cloned.1.call-done = bf16[128,8,4,128]{3,1,2,0:T(8,128)(2,1)} async-done(((bf16[8,8,4,128]{3,1,2,0:T(8,128)(2,1)}), bf16[128,8,4,128]{3,1,2,0:T(8,128)(2,1)}) %all-gather.6.cloned.1.call-update) | async-done | bytes 1048592 | tf_op jit(solution)/shard_map/all_gather | solution.py:67
  133.6 1.8 copy.184
  135.4 0.4 fusion.15
  135.9 76.6 %all-gather.8.cloned.1.call-done = bf16[128,1024,16]{1,0,2:T(8,128)(2,1)} async-done(((bf16[8,1024,16]{1,0,2:T(8,128)(2,1)}), bf16[128,1024,16]{1,0,2:T(8,128)(2,1)}) %all-gather.8.cloned.1.call-update) | async-done | bytes 4194320 | tf_op jit(solution)/shard_map/all_gather | solution.py:67
  212.5 4.5 copy.188
  217.0 1.4 fusion.36
  218.4 0.1 broadcast_in_dim.89
  218.5 4.7 all_to_all.53
  223.2 0.1 reduce_sum.79
  223.3 0.2 fusion.30
  223.5 0.1 fusion.32
  223.7 0.5 fusion.5
  224.2 0.3 broadcast_in_dim.96
  225.9 117.7 %all_to_all.54 = bf16[128,1,8,1024]{3,2,1,0:T(8,128)(2,1)} all-to-all(bf16[128,1,8,1024]{3,2,1,0:T(8,128)(2,1)S(1)} %constant_dynamic-update-slice_fusion), channel_id=1, replica_groups=mesh['grp'=2,'ep_0'=8,'ep_1'=16,'tp'=2] {'ep_0','ep_1'}, dimensions={0} | all-to-all | bytes 4194304 | tf_op jit(solution)/shard_map/all_to_all | solution.py:192
  343.7 14.4 %all-gather.10.cloned.1.call-done = bf16[1,1024,2048]{2,1,0:T(8,128)(2,1)} async-done(((bf16[1,1024,1024]{2,1,0:T(8,128)(2,1)}), bf16[1,1024,2048]{2,1,0:T(8,128)(2,1)}) %all-gather.10.cloned.1.call-update) | async-done | bytes 4194320 | tf_op jit(solution)/shard_map/all_gather | solution.py:194
  358.1 4.6 fusion.2
  362.7 7.3 %convert_bitcast_fusion = bf16[1,1,1024,2048]{3,2,1,0:T(8,128)(2,1)} fusion(bf16[1,192,2048]{2,1,0:T(8,128)(2,1)S(1)} %copy-done, bf16[1,1024,2048]{2,1,0:T(8,128)(2,1)} %all-gather.10.cloned.1.call-done, bf16[1,2048,192]{1,2,0:T(8,128)(2,1)} %param.24, f32[1024,192]{0,1:T(8,128)} %fusion.2), kind=kOutput, calls=%fused_computation.6 | convolution fusion | flops 1613889536 | bytes 10747904 | tf_op jit(solution)/shard_map/prf,pfd->prd/dot_general | solution.py:112
  370.0 20.6 %copy.194 = bf16[1,1,1024,2048]{2,1,0,3:T(2,128)(2,1)} copy(bf16[1,1,1024,2048]{3,2,1,0:T(8,128)(2,1)} %convert_bitcast_fusion) | data formatting | bytes 8388608 | tf_op jit(solution)/shard_map/broadcast_in_dim | solution.py:196
  390.6 0.5 broadcast.147
  391.1 26.0 %reduce.4 = bf16[2048,1024]{1,0:T(8,128)(2,1)} reduce(bf16[2048,1,1,1024]{3,2,1,0:T(2,128)(2,1)} %bitcast.614, bf16[]{:T(256)} %broadcast.147), dimensions={1,2}, to_apply=%bitcast.597.reduce_sub_computation | reduce | bytes 8388610
  417.0 5.9 reshape.242
  422.9 11.9 %all_to_all.55 = bf16[2,2,524288]{2,1,0:T(2,128)(2,1)} all-to-all(bf16[2,2,524288]{2,1,0:T(2,128)(2,1)} %reshape.242), channel_id=1, replica_groups=mesh['grp'=2,'ep_0'=8,'ep_1'=16,'tp'=2] {'tp'}, dimensions={0} | all-to-all | bytes 8388608 | tf_op jit(solution)/shard_map/all_to_all | solution.py:196
  434.9 7.1 %reshape.243 = bf16[2048,1,1,1024]{3,2,1,0:T(2,128)(2,1)} reshape(bf16[2,2,524288]{2,1,0:T(2,128)(2,1)} %all_to_all.55) | data formatting | bytes 8388608
  441.9 7.1 %copy.200 = bf16[1,1,1024,2048]{2,3,0,1:T(8,128)(2,1)} copy(bf16[1,1,1024,2048]{2,1,0,3:T(2,128)(2,1)} %bitcast.615) | data formatting | bytes 8388608
  449.0 11.3 %copy.195 = bf16[2,1,1024,1024]{3,0,1,2:T(2,128)(2,1)} copy(bf16[2,1,1024,1024]{2,3,0,1:T(8,128)(2,1)} %bitcast.616) | data formatting | bytes 8388608 | tf_op jit(solution)/shard_map/all_to_all | solution.py:196
  460.3 21.4 %all-to-all-start.6 = ((bf16[2,1,1024,1024]{3,0,1,2:T(2,128)(2,1)}), bf16[2,1,1024,1024]{3,0,1,2:T(2,128)(2,1)}, u32[]{:S(2)}, u32[]{:S(2)}) async-start(bf16[2,1,1024,1024]{3,0,1,2:T(2,128)(2,1)} %copy.195), calls=%async_computation.6 | async-start | bytes 8388608 | tf_op jit(solution)/shard_map/all_to_all | solution.py:197
  481.9 0.1 reshape.225
  482.0 0.2 fusion.54
  482.2 2.9 gather_fusion
  485.1 0.1 reshape.228
  485.4 0.2 fusion.34
  485.6 0.1 copy.193
  485.7 0.7 constant_dynamic-slice_fusion
  486.4 186.6 %all-to-all-done.6 = bf16[2,1,1024,1024]{3,0,1,2:T(2,128)(2,1)} async-done(((bf16[2,1,1024,1024]{3,0,1,2:T(2,128)(2,1)}), bf16[2,1,1024,1024]{3,0,1,2:T(2,128)(2,1)}, u32[]{:S(2)}, u32[]{:S(2)}) %all-to-all-start.6) | async-done | bytes 4194336 | tf_op jit(solution)/shard_map/all_to_all | solution.py:197
  673.0 12.4 %convert_reduce_fusion = bf16[1024,1024]{1,0:T(8,128)(2,1)S(1)} fusion(bf16[2,1,1024,1024]{3,0,1,2:T(2,128)(2,1)} %all-to-all-done.6), kind=kLoop, calls=%fused_computation.1 | loop fusion | flops 3145728 | bytes 6291456 | tf_op jit(solution)/shard_map/tk,qkd->td/reduce_sum | solution.py:199
  685.4 1.2 fusion.55
  (170 shorter events, 1.7 us)
Async XLA Ops:
  7.2 355.5 %copy-start = (bf16[1,192,2048]{2,1,0:T(8,128)(2,1)S(1)}, bf16[1,192,2048]{2,1,0:T(8,128)(2,1)}, u32[]{:S(2)}) copy-start(bf16[1,192,2048]{2,1,0:T(8,128)(2,1)} %param.25) | copy-start | bytes 2359300
  7.2 126.4 %all-gather.6.cloned.1.call-start = ((), (), s32[]{:S(2)}) async-start(), calls=%async_computation.7 | async-start | bytes 1114112 | tf_op jit(solution)/shard_map/all_gather | solution.py:67
  34.8 177.6 %all-gather.8.cloned.1.call-start = ((), (), s32[]{:S(2)}) async-start(), calls=%async_computation.8 | async-start | bytes 4456448 | tf_op jit(solution)/shard_map/all_gather | solution.py:67
  63.2 5.4 copy-start.6
  63.2 5.4 copy-start.7
  63.2 6.1 all-to-all-start
  85.8 4.6 copy-start.4
  85.8 7.2 %all-to-all-start.2 = ((f32[2,64,8,513]{3,2,1,0:T(8,128)}), f32[2,64,8,513]{3,2,1,0:T(8,128)S(1)}, u32[]{:S(2)}, u32[]{:S(2)}) async-start(f32[2,64,8,513]{3,2,1,0:T(8,128)} %maximum_bitcast_fusion), calls=%async_computation.2 | async-start | bytes 5242880 | tf_op jit(solution)/shard_map/all_to_all | solution.py:49
  89.8 268.3 %all-gather.10.cloned.1.call-start = ((), (), s32[]{:S(2)}) async-start(), calls=%async_computation.9 | async-start | bytes 6291456 | tf_op jit(solution)/shard_map/all_gather | solution.py:194
  218.5 4.9 copy-start.3
  218.5 5.0 copy-start.5
  343.6 14.5 %copy-start.8 = (bf16[1,2048,192]{1,2,0:T(8,128)(2,1)S(1)}, bf16[1,2048,192]{1,2,0:T(8,128)(2,1)}, u32[]{:S(2)}) copy-start(bf16[1,2048,192]{1,2,0:T(8,128)(2,1)} %param.23) | copy-start | bytes 2359300
  460.3 21.7 %copy-start.2 = (bf16[2048,64]{0,1:T(8,128)(2,1)S(1)}, bf16[2048,64]{0,1:T(8,128)(2,1)}, u32[]{:S(2)}) copy-start(bf16[2048,64]{0,1:T(8,128)(2,1)} %param.21) | copy-start | bytes 786436
  460.3 212.7 %all-to-all-start.6 = ((bf16[2,1,1024,1024]{3,0,1,2:T(2,128)(2,1)}), bf16[2,1,1024,1024]{3,0,1,2:T(2,128)(2,1)}, u32[]{:S(2)}, u32[]{:S(2)}) async-start(bf16[2,1,1024,1024]{3,0,1,2:T(2,128)(2,1)} %copy.195), calls=%async_computation.6 | async-start | bytes 8388608 | tf_op jit(solution)/shard_map/all_to_all | solution.py:197
  673.0 13.6 %copy-start.1 = (bf16[1,192,2048]{2,1,0:T(8,128)(2,1)S(1)}, bf16[1,192,2048]{2,1,0:T(8,128)(2,1)}, u32[]{:S(2)}) copy-start(bf16[1,192,2048]{2,1,0:T(8,128)(2,1)} %param.25) | copy-start | bytes 2359300
Sparse Core Ops, SparseCore 0:
  34.9 98.6 all-gather.5
  135.7 76.6 all-gather.7
  343.8 14.2 all-gather.9
